TPU v7x, 32 devices: a whole 2x2x4 slice. The times are simulated.
32 devices in a mesh: rows: 4 (over z), cols: 8 (over y, x, core).
Axes of the slice: x: 2, y: 2, z: 4, core: 2. Of those that a mesh axis runs over, the one named last changes fastest.
Arguments:
- features: bfloat16 [12288, 128], P(('rows', 'cols')), may hold values from -6 to 6
- seeds: int32 [384], replicated, may hold values from 0 to 12287
Outputs:
- vector: float32 [12288], P(('rows', 'cols'))
All inputs are finite; a program needn't handle non-finite values.
Results may differ from a plain program's by a relative error of at most 0.0013.
Values may be sent and summed in bfloat16 or wider, within the bound.
A program may use at most 128 MiB of HBM per device.

v0:
```python
import math

import jax
import jax.numpy as jnp
from jax import lax
from jax.sharding import PartitionSpec as P

ITERS = 4


def shards(features, seeds):
    n_rows = lax.axis_size("rows")
    n_cols = lax.axis_size("cols")
    seg = features.shape[0]
    width = features.shape[1]
    col_at = lax.axis_index("cols")
    n_points = seg * n_rows * n_cols
    gamma = 4.0 / width
    row_feat = lax.all_gather(features, "cols", axis=0, tiled=True)
    col_feat = lax.all_gather(features, "rows", axis=0, tiled=True)
    row_wide = row_feat.astype(jnp.float32)
    col_wide = col_feat.astype(jnp.float32)
    row_sq = jnp.sum(row_wide * row_wide, axis=1)
    col_sq = jnp.sum(col_wide * col_wide, axis=1)
    n_block_rows = row_feat.shape[0]
    block = math.gcd(n_block_rows, 1024)
    count_blocks = n_block_rows // block

    def tile_rows(index):
        start = index * block
        part = lax.dynamic_slice_in_dim(row_feat, start, block, 0)
        part_sq = lax.dynamic_slice_in_dim(row_sq, start, block, 0)
        gram = lax.dot_general(
            part, col_feat, (((1,), (1,)), ((), ())), preferred_element_type=jnp.float32
        )
        dist = part_sq[:, None] + col_sq[None, :] - 2.0 * gram
        return jnp.exp(-gamma * jnp.maximum(dist, 0.0)).astype(jnp.bfloat16)

    block_ids = jnp.arange(count_blocks, dtype=jnp.int32)
    col_index = (
        jnp.arange(n_rows, dtype=jnp.int32)[:, None] * (n_cols * seg)
        + col_at * seg
        + jnp.arange(seg, dtype=jnp.int32)[None, :]
    ).reshape(-1)
    count = jnp.sum((seeds[None, :] == col_index[:, None]).astype(jnp.float32), axis=1)
    col_vector = (1.0 + 32.0 * count).astype(jnp.bfloat16)
    ones_col = jnp.ones((col_feat.shape[0],), jnp.bfloat16)

    def first_pass(index):
        weights = tile_rows(index)
        return (
            jnp.dot(weights, ones_col, preferred_element_type=jnp.float32),
            jnp.dot(weights, col_vector, preferred_element_type=jnp.float32),
        )

    degree_part, product_part = lax.map(first_pass, block_ids)
    degree_part = degree_part.reshape(-1)
    product_part = product_part.reshape(-1)
    degree, product = (
        lax.psum_scatter(degree_part, "cols", scatter_dimension=0, tiled=True),
        lax.psum_scatter(product_part, "cols", scatter_dimension=0, tiled=True),
    )
    vector = product
    for step in range(ITERS):
        if step > 0:
            vector_bf = col_vector

            def one_pass(index):
                return jnp.dot(tile_rows(index), vector_bf, preferred_element_type=jnp.float32)

            product = lax.psum_scatter(
                lax.map(one_pass, block_ids).reshape(-1), "cols", scatter_dimension=0, tiled=True
            )
        scaled = product / degree
        full = lax.all_gather(scaled, ("rows", "cols"), axis=0, tiled=True)
        mean_mass = jnp.sum(jnp.abs(full)) / n_points
        vector = scaled / mean_mass
        if step + 1 < ITERS:
            grid_vec = full.reshape(n_rows, n_cols, seg)
            picked = lax.dynamic_index_in_dim(grid_vec, col_at, 1, keepdims=False).reshape(-1)
            col_vector = (picked / mean_mass).astype(jnp.bfloat16)
    return vector


def solution(mesh):
    in_specs = (P(("rows", "cols"), None), P())
    out_specs = P(("rows", "cols"))
    return jax.shard_map(shards, mesh=mesh, in_specs=in_specs, out_specs=out_specs, check_vma=False)
```

profile of v0, /device:TPU:0, one launch (start us, length us, event | category | flops | bytes accessed | tf_op | source)
XLA Modules:
  0.0 353.2 jit_solution(17890693780195112790)
XLA Ops:
  0.0 12.2 %all_gather.18 = bf16[3072,128]{1,0:T(8,128)(2,1)S(1)} all-gather(bf16[384,128]{1,0:T(8,128)(2,1)} %param.10), channel_id=1, replica_groups=mesh['rows'=4,'cols'=8] {'cols'}, dimensions={0}, use_global_device_ids=true | all-gather | bytes 884736 | tf_op jit(solution)/shard_map/all_gather | solution.py:19
  13.6 15.2 %all_gather.19 = bf16[1536,128]{1,0:T(8,128)(2,1)S(1)} all-gather(bf16[384,128]{1,0:T(8,128)(2,1)} %param.10), channel_id=1, replica_groups=mesh['rows'=4,'cols'=8] {'rows'}, dimensions={0}, use_global_device_ids=true | all-gather | bytes 491520 | tf_op jit(solution)/shard_map/all_gather | solution.py:20
  33.3 29.4 %while.42 = (s32[]{:T(128)}, f32[3,1024]{1,0:T(4,128)}, f32[3,1024]{1,0:T(4,128)}, s32[3]{0:T(128)}, f32[3072]{0:T(1024)S(1)}, /*index=5*/f32[1536]{0:T(1024)}, ...) while((s32[]{:T(128)}, f32[3,1024]{1,0:T(4,128)}, ...), condition=%wide.region_4.5_spmd, body=%wide.region_3.4_spmd.sunk | while | flops 418381824 | bytes 10147015 | solution.py:56
  35.2 2.7 exponential_convert_fusion.5
  39.5 1.4 dynamic_update_slice.22
  41.7 1.4 dynamic_update_slice.21
  45.0 2.7 exponential_convert_fusion.5
  49.3 1.4 dynamic_update_slice.22
  51.5 1.4 dynamic_update_slice.21
  54.8 2.7 exponential_convert_fusion.5
  59.1 1.4 dynamic_update_slice.22
  61.3 1.4 dynamic_update_slice.21
  64.2 22.4 %all-reduce.5 = (f32[3072]{0:T(1024)S(1)}, f32[3072]{0:T(1024)S(1)}) all-reduce(f32[3072]{0:T(1024)S(1)} %reshape.77, f32[3072]{0:T(1024)S(1)} %reshape.78), channel_id=2, replica_groups=mesh['rows'=4,'cols'=8] {'cols'}, use_global_device_ids=true, to_apply=%region_5.6.clone | all-reduce | flops 6144 | bytes 49152
  88.5 39.4 %all-gather = f32[32,1,384]{2,1,0:T(1,128)S(1)} all-gather(f32[1,1,384]{2,1,0:T(1,128)S(1)} %reshape.85), channel_id=1, replica_groups=mesh['rows'=4,'cols'=8] {'rows','cols'}, dimensions={0}, use_global_device_ids=true | all-gather | bytes 50688 | tf_op jit(solution)/shard_map/all_gather | solution.py:75
  129.3 13.7 %while.43 = (s32[]{:T(128)}, f32[3,1024]{1,0:T(4,128)S(1)}, s32[3]{0:T(128)S(1)}, f32[3072]{0:T(1024)S(1)}, f32[1536]{0:T(1024)}, /*index=5*/bf16[3072,128]{1,0:...) while((s32[]{:T(128)}, f32[3,1024]{1,0:T(4,128)S(1)}, ...), condition=%wide.region_9.10_spmd, body=%wide.region_8.9_spmd.sunk | while | flops 415236096 | bytes 697531 | solution.py:72
  130.7 3.2 fusion.71
  135.2 3.2 fusion.71
  139.8 3.2 fusion.71
  143.1 22.5 %all-reduce.2 = f32[3072]{0:T(1024)S(1)} all-reduce(f32[3072]{0:T(1024)S(1)} %reshape.80), channel_id=4, replica_groups=mesh['rows'=4,'cols'=8] {'cols'}, use_global_device_ids=true, to_apply=%region_10.11.clone | all-reduce | flops 3072 | bytes 24576
  165.7 36.4 %all-gather.1 = f32[32,1,384]{2,1,0:T(1,128)S(1)} all-gather(f32[1,1,384]{2,1,0:T(1,128)S(1)} %reshape.87), channel_id=1, replica_groups=mesh['rows'=4,'cols'=8] {'rows','cols'}, dimensions={0}, use_global_device_ids=true | all-gather | bytes 50688 | tf_op jit(solution)/shard_map/all_gather | solution.py:75
  203.5 13.7 %while.44 = (s32[]{:T(128)}, f32[3,1024]{1,0:T(4,128)S(1)}, s32[3]{0:T(128)S(1)}, f32[3072]{0:T(1024)S(1)}, f32[1536]{0:T(1024)}, /*index=5*/bf16[3072,128]{1,0:...) while((s32[]{:T(128)}, f32[3,1024]{1,0:T(4,128)S(1)}, ...), condition=%wide.region_13.14_spmd, body=%wide.region_12.13_spmd.sunk | while | flops 415236096 | bytes 697531 | solution.py:72
  204.9 3.2 fusion.75
  209.4 3.2 fusion.75
  214.0 3.2 fusion.75
  217.3 22.5 %all-reduce.3 = f32[3072]{0:T(1024)S(1)} all-reduce(f32[3072]{0:T(1024)S(1)} %reshape.82), channel_id=5, replica_groups=mesh['rows'=4,'cols'=8] {'cols'}, use_global_device_ids=true, to_apply=%region_14.15.clone | all-reduce | flops 3072 | bytes 24576
  239.9 37.1 %all-gather.2 = f32[32,1,384]{2,1,0:T(1,128)S(1)} all-gather(f32[1,1,384]{2,1,0:T(1,128)S(1)} %reshape.89), channel_id=1, replica_groups=mesh['rows'=4,'cols'=8] {'rows','cols'}, dimensions={0}, use_global_device_ids=true | all-gather | bytes 50688 | tf_op jit(solution)/shard_map/all_gather | solution.py:75
  278.4 13.7 %while.45 = (s32[]{:T(128)}, f32[3,1024]{1,0:T(4,128)S(1)}, s32[3]{0:T(128)S(1)}, f32[3072]{0:T(1024)S(1)}, f32[1536]{0:T(1024)}, /*index=5*/bf16[3072,128]{1,0:...) while((s32[]{:T(128)}, f32[3,1024]{1,0:T(4,128)S(1)}, ...), condition=%wide.region_17.18_spmd, body=%wide.region_16.17_spmd.sunk | while | flops 415236096 | bytes 697531 | solution.py:72
  279.7 3.2 fusion.79
  284.3 3.2 fusion.79
  288.8 3.2 fusion.79
  292.1 22.5 %all-reduce.4 = f32[3072]{0:T(1024)S(1)} all-reduce(f32[3072]{0:T(1024)S(1)} %reshape.84), channel_id=6, replica_groups=mesh['rows'=4,'cols'=8] {'cols'}, use_global_device_ids=true, to_apply=%region_18.19.clone | all-reduce | flops 3072 | bytes 24576
  314.7 36.5 %all-gather.3 = f32[32,1,384]{2,1,0:T(1,128)S(1)} all-gather(f32[1,1,384]{2,1,0:T(1,128)S(1)} %reshape.91), channel_id=1, replica_groups=mesh['rows'=4,'cols'=8] {'rows','cols'}, dimensions={0}, use_global_device_ids=true | all-gather | bytes 50688 | tf_op jit(solution)/shard_map/all_gather | solution.py:75
  (97 shorter events, 30.3 us)
Async XLA Ops:
  12.2 0.9 copy-start
where the time goes:
time: 355 us; the launch traced here: 353 us
  blocking collectives  267 us (75%)
  matrix products  41.9 us (12%)
  local copies, waits for them, and re-layouts  26 us (7%)
  loops' own time  8.07 us (2%)
  other arithmetic  7.08 us (2%)
    all_gather x4, blocking collectives, shards(): full = lax.all_gather(scaled, ('rows', 'cols'), axis=0, tiled=True)  149 us
    unnamed x4, blocking collectives  89.9 us
    dot_general x9, matrix products, one_pass(): jnp.dot(tile_rows(index), vector_bf, preferred_element_type=jnp.float32)  28.4 us
    all_gather x1, blocking collectives, shards(): col_feat = lax.all_gather(features, 'rows', axis=0, tiled=True)  15.2 us
    all_gather x1, blocking collectives, shards(): row_feat = lax.all_gather(features, 'cols', axis=0, tiled=True)  12.2 us
    dynamic_slice x12, local copies, waits for them, and re-layouts, shards(): degree_part, product_part = lax.map(first_pass, block_ids)  9.61 us
    dynamic_update_slice x15, local copies, waits for them, and re-layouts, shards(): degree_part, product_part = lax.map(first_pass, block_ids)  8.77 us
    dot_general x3, matrix products, tile_rows(): lax.dot_general(part, col_feat, (((1,), (1,)), ((), ())), preferred_eleme...  8.03 us

commit v1 on v0

v1 whole, which is shorter than its diff:
```python
import functools

import jax
import jax.numpy as jnp
from jax import lax
from jax.experimental import pallas as pl
from jax.experimental.pallas import tpu as pltpu
from jax.sharding import PartitionSpec as P

ITERS = 4
LANES = 128
MESH = pl.DeviceIdType.MESH


def flip(index, mask):
    bit = 1
    out = index
    while bit <= mask:
        if mask & bit:
            out = out + bit - 2 * bit * ((index // bit) % 2)
        bit *= 2
    return out


def plan(n_rows, n_cols):
    def last_bit(shift, mask):
        if mask & 1:
            return 1
        bits = [1 << k for k in range(n_cols.bit_length()) if mask >> k & 1]
        return bits[shift % len(bits)]

    def key(slot):
        shift, mask = slot
        return 2.1 * shift + 2.1 * bin(mask >> 1).count("1") + 0.5 * (mask & 1)

    slots = sorted(
        ((s, m) for s in range(n_rows) for m in range(n_cols)), key=key
    )
    onward = {slot: [] for slot in slots}
    for shift, mask in slots:
        if mask:
            bit = last_bit(shift, mask)
            onward[(shift, mask ^ bit)].append((bit, (shift, mask)))
    for slot in slots:
        onward[slot].sort(key=lambda item: item[0])
    groups = []
    for at, slot in enumerate(slots):
        if groups and key(slots[groups[-1][0]]) == key(slot) and slot != slots[1]:
            groups[-1].append(at)
        else:
            groups.append([at])
    return slots, onward, groups


def kernel(n_rows, n_cols, feat_ref, seeds_ref, out_ref, feats, weights, lhs, own_sq, seed_rows,
           parts, feat_send, feat_recv, part_send, part_recv):
    seg, width = feat_ref.shape
    slots, onward, groups = plan(n_rows, n_cols)
    at_of = {slot: at for at, slot in enumerate(slots)}
    n_slots = len(slots)
    n_points = n_slots * seg
    gamma = 4.0 / width
    row = lax.axis_index("rows")
    col = lax.axis_index("cols")
    col_bits = [1 << k for k in range(n_cols.bit_length() - 1)]

    def device(shift, mask):
        return ((row + n_rows - shift) % n_rows, flip(col, mask))

    barrier = pltpu.get_barrier_semaphore()
    near = [device(s, 0) for s in range(1, n_rows)] + [device(0, b) for b in col_bits]
    for peer in near:
        pl.semaphore_signal(barrier, inc=1, device_id=peer, device_id_type=MESH)

    own = feat_ref[...]
    wide = own.astype(jnp.float32)
    sq = jnp.sum(wide * wide, axis=1, keepdims=True)
    own_sq[...] = jnp.transpose(jnp.broadcast_to(sq, (seg, LANES)))[:8]
    for q in range(seeds_ref.shape[0]):
        seed_rows[pl.ds(q * LANES, LANES), :] = jnp.transpose(
            jnp.broadcast_to(seeds_ref[q : q + 1, :], (LANES, LANES))
        )
    feats[0] = own
    pl.semaphore_wait(barrier, len(near))

    def hop(source, target_at, peer):
        return pltpu.make_async_remote_copy(
            src_ref=source,
            dst_ref=feats.at[target_at],
            send_sem=feat_send.at[target_at],
            recv_sem=feat_recv.at[target_at],
            device_id=peer,
            device_id_type=MESH,
        )

    sent = []

    def send_on(slot):
        source = feat_ref if slot == (0, 0) else feats.at[at_of[slot]]
        hops = [(device(0, bit), target) for bit, target in onward[slot]]
        if slot == (0, 0):
            hops += [(device(s, 0), (s, 0)) for s in range(1, n_rows)]
        for peer, target in hops:
            copy = hop(source, at_of[target], peer)
            copy.start()
            sent.append(copy)

    def start_row(at):
        shift, mask = slots[at]
        base = (((row + shift) % n_rows) * n_cols + flip(col, mask)) * seg
        for k in range(seg // LANES):
            index = base + k * LANES + lax.broadcasted_iota(jnp.int32, (1, LANES), 1)
            hit = (seed_rows[...] == index).astype(jnp.float32)
            start = 1.0 + 32.0 * jnp.sum(hit, axis=0, keepdims=True)
            first = lax.broadcasted_iota(jnp.int32, (8, LANES), 0) == 0
            lhs[at, :, k * LANES : (k + 1) * LANES] = jnp.where(first, start, 1.0)

    def block(at, total):
        part = feats[at]
        gram = lax.dot_general(
            part, feat_ref[...], (((1,), (1,)), ((), ())), preferred_element_type=jnp.float32
        )
        part_wide = part.astype(jnp.float32)
        part_sq = jnp.sum(part_wide * part_wide, axis=1, keepdims=True)
        dist = part_sq + own_sq[0:1, :] - 2.0 * gram
        value = jnp.exp(-gamma * jnp.maximum(dist, 0.0)).astype(jnp.bfloat16)
        weights[at] = value
        return total + jnp.dot(
            lhs[at].astype(jnp.bfloat16), value, preferred_element_type=jnp.float32
        )

    total = jnp.zeros((8, seg), jnp.float32)
    send_on((0, 0))
    for at in range(n_slots):
        start_row(at)
    for group in groups:
        for at in group:
            if at:
                hop(feat_ref, at, device(0, 1)).wait_recv()
                send_on(slots[at])
        total = lax.fori_loop(group[0], group[-1] + 1, block, total)
    for copy in sent:
        copy.wait_send()

    degree = total[1:2, :]
    product = total[0:1, :]
    step_slots = 4 if n_slots % 4 == 0 else 1
    for step in range(ITERS):
        if step > 0:
            def multiply(at, acc):
                for k in range(step_slots):
                    one = at * step_slots + k
                    row_vec = parts[step - 1, one] / mean
                    left = jnp.broadcast_to(row_vec, (8, seg)).astype(jnp.bfloat16)
                    acc = acc + jnp.dot(left, weights[one], preferred_element_type=jnp.float32)
                return acc

            product = lax.fori_loop(
                0, n_slots // step_slots, multiply, jnp.zeros((8, seg), jnp.float32)
            )[0:1, :]
        scaled = product / degree
        parts[step, 0] = scaled
        for at in range(1, n_slots):
            pltpu.make_async_remote_copy(
                src_ref=parts.at[step, 0],
                dst_ref=parts.at[step, at],
                send_sem=part_send.at[step],
                recv_sem=part_recv.at[step],
                device_id=device(*slots[at]),
                device_id_type=MESH,
            ).start()
        rest = parts.at[step, pl.ds(1, n_slots - 1)]
        pltpu.make_async_copy(rest, rest, part_recv.at[step]).wait()
        mean = jnp.sum(jnp.abs(parts[step])) / n_points
    out_ref[...] = scaled / mean
    for step in range(ITERS):
        rest = parts.at[step, pl.ds(1, n_slots - 1)]
        pltpu.make_async_copy(rest, rest, part_send.at[step]).wait()


def shards(features, seeds):
    n_rows = lax.axis_size("rows")
    n_cols = lax.axis_size("cols")
    seg, width = features.shape
    n_slots = n_rows * n_cols
    pad = -seeds.shape[0] % LANES
    seeds = jnp.pad(seeds, (0, pad), constant_values=-1).reshape(-1, LANES)
    vmem = pl.BlockSpec(memory_space=pltpu.VMEM)
    out = pl.pallas_call(
        functools.partial(kernel, n_rows, n_cols),
        out_shape=jax.ShapeDtypeStruct((1, seg), jnp.float32),
        in_specs=[vmem, vmem],
        out_specs=vmem,
        scratch_shapes=[
            pltpu.VMEM((n_slots, seg, width), jnp.bfloat16),
            pltpu.VMEM((n_slots, seg, seg), jnp.bfloat16),
            pltpu.VMEM((n_slots, 8, seg), jnp.float32),
            pltpu.VMEM((8, seg), jnp.float32),
            pltpu.VMEM((seeds.shape[0] * LANES, LANES), jnp.int32),
            pltpu.VMEM((ITERS, n_slots, 1, seg), jnp.float32),
            pltpu.SemaphoreType.DMA((n_slots,)),
            pltpu.SemaphoreType.DMA((n_slots,)),
            pltpu.SemaphoreType.DMA((ITERS,)),
            pltpu.SemaphoreType.DMA((ITERS,)),
        ],
        compiler_params=pltpu.CompilerParams(
            collective_id=0, has_side_effects=True, vmem_limit_bytes=67043328
        ),
    )(features, seeds)
    return out.reshape(seg)


def solution(mesh):
    in_specs = (P(("rows", "cols"), None), P())
    out_specs = P(("rows", "cols"))
    return jax.shard_map(shards, mesh=mesh, in_specs=in_specs, out_specs=out_specs, check_vma=False)
```

time: 355 us -> 61.5 us (0.17)
  blocking collectives: 267 us -> 0 us
  Pallas kernels: 0 us -> 60.1 us
  matrix products: 41.9 us -> 0 us
  local copies, waits for them, and re-layouts: 26 us -> 0 us
  loops' own time: 8.07 us -> 0 us
  other arithmetic: 7.08 us -> 1.28 us
    all_gather x6 -> x0, blocking collectives: 177 us -> none  [the longest x4 149 us: shards(): full = lax.all_gather(scaled, ('rows', 'cols'), axis=0, tiled=True)]
    unnamed x4 -> x0, blocking collectives: 89.9 us -> none
    pallas_call x0 -> x1, Pallas kernels: none -> 60.1 us  [shards(): pl.pallas_call(functools.partial(kernel, n_rows, n_cols), out_shape=jax.S...]
    dot_general x18 -> x0, matrix products: 41.9 us -> none  [the longest x9 28.4 us: one_pass(): jnp.dot(tile_rows(index), vector_bf, preferred_element_type=jnp.float32)]
    dynamic_slice x24 -> x0, local copies, waits for them, and re-layouts: 9.71 us -> none  [the longest x12 9.61 us: shards(): degree_part, product_part = lax.map(first_pass, block_ids)]
    dynamic_update_slice x15 -> x0, local copies, waits for them, and re-layouts: 8.77 us -> none  [shards(): degree_part, product_part = lax.map(first_pass, block_ids)]
    another operation x4 -> x0, loops' own time: 8.07 us -> none  [the longest x3 6.12 us: shards(): lax.map(one_pass, block_ids).reshape(-1)]
    reduce_sum x7 -> x0, other arithmetic: 5.32 us -> none  [the longest x4 2.8 us: shards(): mean_mass = jnp.sum(jnp.abs(full)) / n_points]
where the time goes in v1:
time: 61.5 us; the launch traced here: 61.4 us
  Pallas kernels  60.1 us (98%)
  other arithmetic  1.28 us (2%)
    pallas_call x1, Pallas kernels, shards(): pl.pallas_call(functools.partial(kernel, n_rows, n_cols), out_shape=jax.S...  60.1 us
    pallas_call x1, other arithmetic, shards(): pl.pallas_call(functools.partial(kernel, n_rows, n_cols), out_shape=jax.S...  1.28 us

profile of v1, /device:TPU:0, one launch (start us, length us, event | category | flops | bytes accessed | tf_op | source)
XLA Modules:
  0.0 61.4 jit_solution(18349917851122993982)
XLA Ops:
  0.0 60.1 %shard_map.28 = f32[1,384]{1,0:T(1,128)} custom-call(bf16[384,128]{1,0:T(8,128)(2,1)} %feat_ref.1, s32[3,128]{1,0:T(4,128)} %bitcast.1), custom_call_target="tpu_custom_call" | custom-call | tf_op jit(solution)/shard_map/pallas_call | solution.py:189
  60.1 1.3 %reduce = f32[384]{0:T(512)} reduce(f32[1,384]{1,0:T(1,128)} %shard_map.28, f32[]{:T(128)} %constant), dimensions={0}, to_apply=%pallas_call.3.reduce_sub_computation | reduce | bytes 3076 | tf_op jit(solution)/shard_map/pallas_call | solution.py:189

commit v2 on v1

--- a/solution.py
+++ b/solution.py
@@ -1,4 +1,5 @@
 import functools
+import math
 
 import jax
 import jax.numpy as jnp
@@ -31,7 +32,7 @@
 
     def key(slot):
         shift, mask = slot
-        return 2.1 * shift + 2.1 * bin(mask >> 1).count("1") + 0.5 * (mask & 1)
+        return 0.2 * shift + 2.1 * bin(mask >> 1).count("1") + 4.3 * (mask & 1)
 
     slots = sorted(
         ((s, m) for s in range(n_rows) for m in range(n_cols)), key=key
@@ -43,16 +44,14 @@
             onward[(shift, mask ^ bit)].append((bit, (shift, mask)))
     for slot in slots:
         onward[slot].sort(key=lambda item: item[0])
-    groups = []
-    for at, slot in enumerate(slots):
-        if groups and key(slots[groups[-1][0]]) == key(slot) and slot != slots[1]:
-            groups[-1].append(at)
-        else:
-            groups.append([at])
+    size = max(n_rows // 2, 1)
+    groups = [[0]] + [
+        list(range(at, min(at + size, len(slots)))) for at in range(1, len(slots), size)
+    ]
     return slots, onward, groups
 
 
-def kernel(n_rows, n_cols, feat_ref, seeds_ref, out_ref, feats, weights, lhs, own_sq, seed_rows,
+def kernel(n_rows, n_cols, feat_ref, seeds_ref, out_ref, feats, weights, lhs, own_scaled, own_sq, seed_rows,
            parts, feat_send, feat_recv, part_send, part_recv):
     seg, width = feat_ref.shape
     slots, onward, groups = plan(n_rows, n_cols)
@@ -75,7 +74,8 @@
     own = feat_ref[...]
     wide = own.astype(jnp.float32)
     sq = jnp.sum(wide * wide, axis=1, keepdims=True)
-    own_sq[...] = jnp.transpose(jnp.broadcast_to(sq, (seg, LANES)))[:8]
+    own_scaled[...] = (wide * (2.0 * gamma)).astype(jnp.bfloat16)
+    own_sq[...] = -gamma * jnp.transpose(jnp.broadcast_to(sq, (seg, LANES)))[:8]
     for q in range(seeds_ref.shape[0]):
         seed_rows[pl.ds(q * LANES, LANES), :] = jnp.transpose(
             jnp.broadcast_to(seeds_ref[q : q + 1, :], (LANES, LANES))
@@ -99,7 +99,7 @@
         source = feat_ref if slot == (0, 0) else feats.at[at_of[slot]]
         hops = [(device(0, bit), target) for bit, target in onward[slot]]
         if slot == (0, 0):
-            hops += [(device(s, 0), (s, 0)) for s in range(1, n_rows)]
+            hops = [(device(s, 0), (s, 0)) for s in range(1, n_rows)] + hops
         for peer, target in hops:
             copy = hop(source, at_of[target], peer)
             copy.start()
@@ -115,45 +115,59 @@
             first = lax.broadcasted_iota(jnp.int32, (8, LANES), 0) == 0
             lhs[at, :, k * LANES : (k + 1) * LANES] = jnp.where(first, start, 1.0)
 
-    def block(at, total):
-        part = feats[at]
-        gram = lax.dot_general(
-            part, feat_ref[...], (((1,), (1,)), ((), ())), preferred_element_type=jnp.float32
+    def add_product(at, total):
+        return total + jnp.dot(
+            lhs[at].astype(jnp.bfloat16), weights[at], preferred_element_type=jnp.float32
         )
-        part_wide = part.astype(jnp.float32)
-        part_sq = jnp.sum(part_wide * part_wide, axis=1, keepdims=True)
-        dist = part_sq + own_sq[0:1, :] - 2.0 * gram
-        value = jnp.exp(-gamma * jnp.maximum(dist, 0.0)).astype(jnp.bfloat16)
-        weights[at] = value
-        return total + jnp.dot(
-            lhs[at].astype(jnp.bfloat16), value, preferred_element_type=jnp.float32
-        )
+
+    def block(at, total, lag):
+        if lag:
+            total = add_product(at - 1, total)
+        for k in range(0, seg, LANES):
+            part = feats[at, k : k + LANES, :]
+            gram = lax.dot_general(
+                part, own_scaled[...], (((1,), (1,)), ((), ())), preferred_element_type=jnp.float32
+            )
+            part_wide = part.astype(jnp.float32)
+            part_sq = -gamma * jnp.sum(part_wide * part_wide, axis=1, keepdims=True)
+            exponent = (part_sq + own_sq[0:1, :]) + gram
+            weights[at, k : k + LANES, :] = jnp.exp(jnp.minimum(exponent, 0.0)).astype(
+                jnp.bfloat16
+            )
+        return total
 
     total = jnp.zeros((8, seg), jnp.float32)
     send_on((0, 0))
-    for at in range(n_slots):
-        start_row(at)
     for group in groups:
         for at in group:
             if at:
                 hop(feat_ref, at, device(0, 1)).wait_recv()
                 send_on(slots[at])
-        total = lax.fori_loop(group[0], group[-1] + 1, block, total)
+        for at in group:
+            start_row(at)
+        if group[0] == 0:
+            total = block(0, total, False)
+            group = group[1:]
+        if group:
+            total = lax.fori_loop(
+                group[0], group[-1] + 1, functools.partial(block, lag=True), total
+            )
+    total = add_product(n_slots - 1, total)
     for copy in sent:
         copy.wait_send()
 
     degree = total[1:2, :]
     product = total[0:1, :]
-    step_slots = 4 if n_slots % 4 == 0 else 1
+    step_slots = math.gcd(n_slots, 8)
     for step in range(ITERS):
         if step > 0:
             def multiply(at, acc):
-                for k in range(step_slots):
-                    one = at * step_slots + k
-                    row_vec = parts[step - 1, one] / mean
-                    left = jnp.broadcast_to(row_vec, (8, seg)).astype(jnp.bfloat16)
-                    acc = acc + jnp.dot(left, weights[one], preferred_element_type=jnp.float32)
-                return acc
+                left = jnp.concatenate(
+                    [parts[step - 1, at * step_slots + k] / mean for k in range(step_slots)], axis=1
+                )
+                left = jnp.broadcast_to(left, (8, step_slots * seg)).astype(jnp.bfloat16)
+                right = weights[pl.ds(at * step_slots, step_slots)].reshape(step_slots * seg, seg)
+                return acc + jnp.dot(left, right, preferred_element_type=jnp.float32)
 
             product = lax.fori_loop(
                 0, n_slots // step_slots, multiply, jnp.zeros((8, seg), jnp.float32)
@@ -195,6 +209,7 @@
             pltpu.VMEM((n_slots, seg, width), jnp.bfloat16),
             pltpu.VMEM((n_slots, seg, seg), jnp.bfloat16),
             pltpu.VMEM((n_slots, 8, seg), jnp.float32),
+            pltpu.VMEM((seg, width), jnp.bfloat16),
             pltpu.VMEM((8, seg), jnp.float32),
             pltpu.VMEM((seeds.shape[0] * LANES, LANES), jnp.int32),
             pltpu.VMEM((ITERS, n_slots, 1, seg), jnp.float32),

time: 61.5 us -> 59.8 us (0.972)
  Pallas kernels: 60.1 us -> 58.4 us
    pallas_call x1, Pallas kernels: 60.1 us -> 58.4 us  [shards(): pl.pallas_call(functools.partial(kernel, n_rows, n_cols), out_shape=jax.S...]
where the time goes in v2:
time: 59.8 us; the launch traced here: 59.7 us
  Pallas kernels  58.4 us (98%)
  other arithmetic  1.28 us (2%)
    pallas_call x1, Pallas kernels, shards(): pl.pallas_call(functools.partial(kernel, n_rows, n_cols), out_shape=jax.S...  58.4 us
    pallas_call x1, other arithmetic, shards(): pl.pallas_call(functools.partial(kernel, n_rows, n_cols), out_shape=jax.S...  1.28 us

profile of v2, /device:TPU:0, one launch (start us, length us, event | category | flops | bytes accessed | tf_op | source)
XLA Modules:
  0.0 59.7 jit_solution(6895068554304513478)
XLA Ops:
  0.0 58.4 %shard_map.28 = f32[1,384]{1,0:T(1,128)} custom-call(bf16[384,128]{1,0:T(8,128)(2,1)} %feat_ref.1, s32[3,128]{1,0:T(4,128)} %bitcast.1), custom_call_target="tpu_custom_call" | custom-call | tf_op jit(solution)/shard_map/pallas_call | solution.py:203
  58.4 1.3 %reduce = f32[384]{0:T(512)} reduce(f32[1,384]{1,0:T(1,128)} %shard_map.28, f32[]{:T(128)} %constant), dimensions={0}, to_apply=%pallas_call.3.reduce_sub_computation | reduce | bytes 3076 | tf_op jit(solution)/shard_map/pallas_call | solution.py:203
